TPU v7x, 32 devices: a whole 2x2x4 slice. The times are simulated.
32 devices in a mesh: sub: 8 (over z, x), grp: 4 (over y, core).
Axes of the slice: x: 2, y: 2, z: 4, core: 2. Of those that a mesh axis runs over, the one named last changes fastest.
Arguments:
- solution: float32 [32, 128, 2048], P(('sub', 'grp')), may hold values from -6 to 6
- residual: float32 [32, 128, 2048], P(('sub', 'grp'))
- direction: float32 [32, 128, 2048], P(('sub', 'grp'))
- residual_product: float32 [128], replicated, may hold values from 65536 to 1310720
- neighbor_slots: int32 [32, 4], P(('sub', 'grp')), may hold values from 0 to 3, each once within a row
- coupling: bfloat16 [32, 96, 256, 128], P(('sub', 'grp')), may hold values from -0.375 to 0.375
- dirichlet_factor: bfloat16 [32, 96, 128, 128], P(('sub', 'grp')), may hold values from -0.5 to 0.5
- face_block: bfloat16 [32, 32, 128, 128], P(('sub', 'grp')), as said below
- neumann_factor: bfloat16 [32, 32, 128, 128], P(('sub', 'grp')), may hold values from -0.5 to 0.5
- primal_block: int32 [32, 128], P(('sub', 'grp')), may hold values from 0 to 31
- primal_basis: bfloat16 [32, 128, 128], P(('sub', 'grp')), may hold values from -1.5 to 1.5
- coarse_matrix: float32 [32, 9, 128, 128], P(('sub', 'grp')), may hold values from -0.17677669 to 0.17677669
- coarse_block_inverse: float32 [32, 128, 128], P(('sub', 'grp')), may hold values from -0.5 to 0.5
- coarse_pattern: int32 [32, 9], P(('sub', 'grp')), may hold values from 0 to 31, as said below
Outputs:
- new_solution: float32 [32, 128, 2048], P(('sub', 'grp'))
- new_residual: float32 [32, 128, 2048], P(('sub', 'grp'))
- new_direction: float32 [32, 128, 2048], P(('sub', 'grp'))
- new_product: float32 [128], replicated
Inputs may be any that keep to these rules, and one draw needn't show every extreme that they name: `neighbor_slots`: each row orders the four local face slots: entry d is the slot of the face toward direction d (sub lower, sub upper, grp lower, grp upper). `coarse_pattern`: row t names 9 different subdomains, the first of them t itself; subdomain s lies on the device of index s along sub+grp, and every entry lies within 2 positions of row t along sub, cyclically. `face_block`: each block is symmetric with every eigenvalue at least 0.5.
All inputs are finite; a program needn't handle non-finite values.
Results may differ from a plain program's by a relative error of at most 0.0003.
Values sent between devices are 32-bit elements; how exact they have to be, the bound alone decides.
A program may use at most 128 MiB of HBM per device.

v0:
```python
import functools

import jax
import jax.numpy as jnp
from jax import lax
from jax.experimental import pallas as pl
from jax.experimental.pallas import tpu as pltpu
from jax.sharding import PartitionSpec as P

REACH = 2
WINDOW = 2 * REACH + 1
MESH = pl.DeviceIdType.MESH
F32 = jnp.float32
BF16 = jnp.bfloat16
NN = (((1,), (0,)), ((), ()))
NT = (((1,), (1,)), ((), ()))


def split(value):
    high = value.astype(BF16)
    low = (value - high.astype(F32)).astype(BF16)
    return jnp.concatenate([high, low], 0)


def merge(value):
    half = value.shape[0] // 2
    return value[:half] + value[half:]


def dot(lhs, rhs, dims=NN):
    return lax.dot_general(lhs, rhs, dims, preferred_element_type=F32)


def exact(lhs, rhs):
    return lax.dot_general(
        lhs, rhs, NN, preferred_element_type=F32, precision=lax.Precision.HIGHEST
    )


def row_sums(value):
    return jnp.sum(value.T, axis=0, keepdims=True)


def as_columns(row, width):
    return jnp.broadcast_to(row, (width, row.shape[1])).T


def kernel(
    n_sub, n_grp,
    sol_h, res_h, dir_h, rp_ref, slots, coup_h, diri_h, face_h, neum_h, pb_ref, basis_h,
    cmat_h, cinv_h, pattern,
    osol_h, ores_h, odir_h, oprod,
    inv_s, U, R, Uhl, V, B, Y, RY, Hhl, H, LS, NXs, NXr, S, OD, Cw, Fd, Fb, Nf, basis, basisx,
    cmat, cinv, Wn, acc, cr2, crn2, crn, rcr, rel, RB, RP, SP, RC, corr, red_g, red_s, red_g2, red_s2, crs,
    stepb, csem, snd, rcv,
):
    ms = lax.axis_index("sub")
    mg = lax.axis_index("grp")
    width = basis.shape[0]
    nb = Fb.shape[0]
    fb = nb // 4
    n_q = Cw.shape[0] // nb
    counter = [0]
    pending = []

    def sub_at(offset):
        return (lax.rem(ms + offset + n_sub, n_sub), mg)

    def grp_at(offset):
        return (ms, lax.rem(mg + offset + n_grp, n_grp))

    def send(src, dst, device):
        i = counter[0]
        counter[0] += 1
        copy = pltpu.make_async_remote_copy(
            src_ref=src, dst_ref=dst, send_sem=snd.at[i], recv_sem=rcv.at[i],
            device_id=device, device_id_type=MESH,
        )
        copy.start()
        pending.append(copy)
        return copy

    def blocks(ref, d):
        return ref.at[pl.ds(d * fb, fb)]

    def columns(ref, half, k):
        return ref.at[0, :, pl.ds((half * fb + k) * width, width)]

    def fetch_face(hbm, half, buf, d, sem):
        for k in range(fb):
            pltpu.make_async_copy(columns(hbm, half, k), buf.at[d * fb + k], csem.at[sem]).start()

    def wait_face(buf, d, sem):
        pltpu.make_async_copy(blocks(buf, d), blocks(buf, d), csem.at[sem]).wait()

    def store_face(buf, d, hbm, half, sem):
        for k in range(fb):
            pltpu.make_async_copy(buf.at[d * fb + k], columns(hbm, half, k), csem.at[sem]).start()

    fetch_face(dir_h, 0, U, 1, 0)
    fetch_face(dir_h, 1, U, 3, 1)
    weight_copies = []
    for s in range(4):
        group = []
        for q in range(n_q):
            part = pl.ds(q * nb + s * fb, fb)
            group.append(pltpu.make_async_copy(coup_h.at[0, part], Cw.at[part], csem.at[10 + 7 * s + q]))
            group.append(pltpu.make_async_copy(diri_h.at[0, part], Fd.at[part], csem.at[10 + 7 * s + 3 + q]))
        part = pl.ds(s * fb, fb)
        group.append(pltpu.make_async_copy(face_h.at[0, part], Fb.at[part], csem.at[10 + 7 * s + 6]))
        weight_copies.append(group)

    barrier = pltpu.get_barrier_semaphore()
    for o in range(1, n_sub):
        pl.semaphore_signal(barrier, inc=1, device_id=sub_at(o), device_id_type=MESH)
    for o in range(1, n_grp):
        pl.semaphore_signal(barrier, inc=1, device_id=grp_at(o), device_id_type=MESH)
    for c in weight_copies[0]:
        c.start()
    fetch_face(res_h, 0, R, 1, 2)
    fetch_face(res_h, 1, R, 3, 3)
    small = [
        pltpu.make_async_copy(basis_h.at[0], basis, csem.at[4]),
        pltpu.make_async_copy(cmat_h.at[0], cmat, csem.at[5]),
        pltpu.make_async_copy(cinv_h.at[0], cinv, csem.at[6]),
        pltpu.make_async_copy(neum_h.at[0], Nf, csem.at[7]),
    ]
    small[0].start()
    small[3].start()
    for group in weight_copies[1:]:
        for c in group:
            c.start()
    for c in small[1:3]:
        c.start()
    fetch_face(sol_h, 0, S, 0, 8)
    fetch_face(sol_h, 1, S, 1, 9)
    pl.semaphore_wait(barrier, n_sub + n_grp - 2)

    wait_face(U, 1, 0)
    u_sub = send(blocks(U, 1), blocks(U, 0), sub_at(1))
    wait_face(U, 3, 1)
    u_grp = send(blocks(U, 3), blocks(U, 2), grp_at(1))
    small[3].wait()
    for side in range(2):
        def widen(k, carry, side=side):
            NXs[side * fb + k] = Nf[slots[0, 2 * side] * fb + k].astype(F32)
            return carry
        lax.fori_loop(0, fb, widen, 0, unroll=2)

    small[0].wait()
    basisx[...] = basis[...].astype(F32)
    primal = pb_ref[...].astype(F32)
    for side in range(2):
        SP[side] = primal - (slots[0, 2 * side] * fb).astype(F32)
    for s in range(4):
        at = jnp.int32(0)
        for d in range(4):
            at = jnp.where(slots[0, d] == s, jnp.int32(d * fb), at)
        inv_s[s] = at
    acc[...] = jnp.zeros_like(acc)

    u_grp.wait_recv()
    u_sub.wait_recv()
    extra = []
    for side, device in ((0, sub_at(-1)), (1, grp_at(-1))):
        extra.append(send(blocks(NXs, side), blocks(NXr, side), device))
        extra.append(send(basisx, RB.at[side], device))
        extra.append(send(SP.at[side], RP.at[side], device))

    for s in range(4):
        def prepare(k, carry, s=s):
            Uhl[s * fb + k] = split(U[inv_s[s] + k])
            return carry
        lax.fori_loop(0, fb, prepare, 0, unroll=2)

    for s in range(4):
        for c in weight_copies[s]:
            c.wait()

        def interior(k, carry, s=s):
            j = s * fb + k
            uj = Uhl[j]
            v = merge(dot(uj, Fb[j]))
            V[j] = v
            total = U[inv_s[s] + k] * v
            for q in range(n_q):
                m = lax.rem(j + q + 1, nb)
                n = q * nb + j
                a = merge(dot(jnp.concatenate([uj, Uhl[m]], 1), Cw[n]))
                t = merge(dot(split(a), Fd[n]))
                total = total + t * t
                B[n] = split(merge(dot(split(t), Fd[n], NT)))
            acc[...] += total
            return carry
        lax.fori_loop(0, fb, interior, 0, unroll=2)

    def reduce_start(row, red, first, index, count, at):
        red[index] = row
        return [send(red.at[index], red.at[index], at(o)) for o in range(1, count)]

    def reduce_end(copies, red, count):
        for c in copies:
            c.wait_recv()
        for c in copies:
            c.wait_send()
            pending[:] = [other for other in pending if other is not c]
        total = red[0]
        for i in range(1, count):
            total = total + red[i]
        return total

    copies = reduce_start(row_sums(acc[...]), red_g, True, mg, n_grp, grp_at)

    def returned(d):
        def body(k, carry):
            j = slots[0, d] * fb + k
            lhs = []
            rhs = []
            for q in range(n_q):
                n = q * nb + j
                p = q * nb + lax.rem(j - q - 1 + nb, nb)
                lhs += [B[n], B[p]]
                rhs += [Cw[n, :width], Cw[p, width:]]
            y = merge(dot(jnp.concatenate(lhs, 1), jnp.concatenate(rhs, 1), NT))
            Y[d * fb + k] = y + V[j]
            return carry
        lax.fori_loop(0, fb, body, 0, unroll=2)

    returned(0)
    part = reduce_end(copies, red_g, n_grp)
    copies = reduce_start(part, red_s, True, ms, n_sub, sub_at)
    ys = {}
    ys[1] = send(blocks(Y, 0), blocks(RY, 1), sub_at(-1))
    returned(2)
    ys[3] = send(blocks(Y, 2), blocks(RY, 3), grp_at(-1))
    returned(1)
    returned(3)
    curvature = reduce_end(copies, red_s, n_sub)
    rp = rp_ref[...]
    stepb[...] = as_columns(rp / curvature, width)

    wait_face(S, 0, 8)
    wait_face(S, 1, 9)
    for half in range(2):
        def iterate(k, carry, half=half):
            S[half * fb + k] = S[half * fb + k] + stepb[...] * U[(2 * half + 1) * fb + k]
            return carry
        lax.fori_loop(0, fb, iterate, 0, unroll=2)
        store_face(S, half, osol_h, half, 8 + half)

    for c in extra:
        c.wait_recv()
    for c in small[1:3]:
        c.wait()
    wait_face(R, 1, 2)
    wait_face(R, 3, 3)
    for side in range(2):
        rel[side] = as_columns(RP[side], width)
    pbc = as_columns(primal, width)
    cr2[...] = jnp.zeros_like(cr2)
    acc[...] = jnp.zeros_like(acc)
    basis32 = basisx[...]

    def pick(j):
        return jnp.where(pbc == j.astype(F32), basis32, 0.0).astype(BF16)

    def pick_other(side, k):
        return jnp.where(rel[side] == k.astype(F32), RB[side], 0.0).astype(BF16)

    def residual_face(d):
        side = d // 2
        ys[d].wait_recv()
        crn2[...] = jnp.zeros_like(crn2)

        def body(k, carry):
            i = d * fb + k
            new = R[i] - stepb[...] * (Y[i] + RY[i])
            H[i] = new
            hl = split(new * 0.5)
            Hhl[i] = hl
            cr2[...] += dot(hl, pick(slots[0, d] * fb + k), NT)
            crn2[...] += dot(hl, pick_other(side, k), NT)
            return carry
        lax.fori_loop(0, fb, body, 0, unroll=2)
        crn[side] = merge(crn2[...])
        store_face(H, d, ores_h, side, side)

    def local_face(d):
        side = d // 2

        def body(k, carry):
            i = d * fb + k
            hl = Hhl[i]
            factor = Nf[slots[0, d] * fb + k]
            other = NXr[side * fb + k].astype(BF16)
            t = merge(dot(hl, factor))
            w = merge(dot(hl, other))
            acc[...] += t * t + w * w
            LS[i] = 0.5 * (merge(dot(split(t), factor, NT)) + merge(dot(split(w), other, NT)))
            return carry
        lax.fori_loop(0, fb, body, 0, unroll=2)

    residual_face(3)
    cr_grp = send(crn.at[1], rcr.at[1], grp_at(1))
    residual_face(1)
    cr_sub = send(crn.at[0], rcr.at[0], sub_at(1))
    local_face(3)
    cr_grp.wait_recv()
    cr_sub.wait_recv()
    cr = merge(cr2[...]) + rcr[0] + rcr[1]
    crs[...] = cr
    first = exact(cr, cinv[...])

    def place(g, p):
        return Wn.at[g * WINDOW + p]

    Wn[mg * WINDOW + REACH] = first
    arrivals = {}
    for o in (1, -1, 2, -2):
        p = REACH - o
        arrivals[p] = send(place(mg, REACH), place(mg, p), sub_at(o))
    order = (REACH, REACH - 2, REACH + 2, REACH - 1, REACH + 1)
    if n_grp == 4:
        near = (ms, mg + 1 - 2 * lax.rem(mg, 2))
        far = lax.rem(mg + 2, 4)
        far_copies = {}
        column_copies = []

        def pass_on(p):
            far_copies[p] = send(place(mg, p), place(mg, p), (ms, far))
            column_copies.append(send(place(mg, p), place(mg, p), near))
        pass_on(REACH)
        local_face(1)
        for p in order[1:]:
            arrivals[p].wait_recv()
            pass_on(p)
        for p in order:
            far_copies[p].wait_recv()
            column_copies.append(send(place(far, p), place(far, p), near))
        for c in column_copies:
            c.wait_recv()
    else:
        column_copies = []
        local_face(1)
        for p in order:
            if p != REACH:
                arrivals[p].wait_recv()
            for o in range(1, n_grp):
                column_copies.append(send(place(mg, p), place(mg, p), grp_at(o)))
        for c in column_copies:
            c.wait_recv()

    chosen = []
    for k in range(cmat.shape[0]):
        entry = pattern[0, k]
        p = lax.min(lax.rem(entry // n_grp - ms + REACH + n_sub, n_sub), jnp.int32(WINDOW - 1))
        chosen.append(Wn[lax.rem(entry, n_grp) * WINDOW + p])
    adjacent = exact(
        jnp.concatenate(chosen, 1), cmat[...].reshape(cmat.shape[0] * width, width)
    )
    correction = Wn[mg * WINDOW + REACH] + exact(crs[...] - adjacent, cinv[...])
    corr[...] = correction
    c_sub = send(corr, RC.at[0], sub_at(-1))
    c_grp = send(corr, RC.at[1], grp_at(-1))
    product_row = row_sums(acc[...] + correction * crs[...])
    copies = reduce_start(product_row, red_g2, False, mg, n_grp, grp_at)

    corr_hl = split(correction * 0.5)

    def own_spread(d):
        def body(k, carry):
            i = d * fb + k
            LS[i] = LS[i] + merge(dot(corr_hl, pick(slots[0, d] * fb + k)))
            return carry
        lax.fori_loop(0, fb, body, 0, unroll=2)

    own_spread(1)
    part = reduce_end(copies, red_g2, n_grp)
    copies = reduce_start(part, red_s2, False, ms, n_sub, sub_at)
    own_spread(3)

    def borrowed_spread(side):
        d = 2 * side + 1
        other_hl = split(RC[side] * 0.5)

        def body(k, carry):
            i = d * fb + k
            rows = pick_other(side, k)
            OD[side * fb + k] = LS[i] + merge(dot(other_hl, rows))
            return carry
        lax.fori_loop(0, fb, body, 0, unroll=2)

    c_grp.wait_recv()
    borrowed_spread(1)
    c_sub.wait_recv()
    borrowed_spread(0)
    product = reduce_end(copies, red_s2, n_sub)
    oprod[...] = product
    ratio = as_columns(product / rp, width)
    for half in range(2):
        def advance(k, carry, half=half):
            OD[half * fb + k] = OD[half * fb + k] + ratio * U[(2 * half + 1) * fb + k]
            return carry
        lax.fori_loop(0, fb, advance, 0, unroll=2)
        store_face(OD, half, odir_h, half, 2 + half)

    for half in range(2):
        wait_face(S, half, 8 + half)
        wait_face(H, 2 * half + 1, half)
        wait_face(OD, half, 2 + half)
    for c in pending:
        c.wait_send()


def shards(
    solution, residual, direction, residual_product, neighbor_slots, coupling,
    dirichlet_factor, face_block, neumann_factor, primal_block, primal_basis,
    coarse_matrix, coarse_block_inverse, coarse_pattern,
):
    n_sub = lax.axis_size("sub")
    n_grp = lax.axis_size("grp")
    loads = direction.shape[1]
    nb = face_block.shape[1]
    width = face_block.shape[2]
    fb = nb // 4
    inner = coupling.shape[1]
    copies = 8 + 4 + 2 + 2 + 4 + 3 * WINDOW + 2 * (n_sub + n_grp) + WINDOW * n_grp
    hbm = pl.BlockSpec(memory_space=pltpu.HBM)
    free = pl.BlockSpec(memory_space=pl.ANY)
    vmem = pl.BlockSpec(memory_space=pltpu.VMEM)
    smem = pl.BlockSpec(memory_space=pltpu.SMEM)

    def block(count, dtype=F32, rows=loads):
        return pltpu.VMEM((count, rows, width), dtype)

    scratch = [
        pltpu.SMEM((4,), jnp.int32),
        block(nb), block(nb), block(nb, BF16, 2 * loads), block(nb),
        block(inner, BF16, 2 * loads), block(nb), block(nb),
        block(nb, BF16, 2 * loads), block(nb), block(nb), block(2 * fb), block(2 * fb),
        block(2 * fb), block(2 * fb),
        pltpu.VMEM(coupling.shape[1:], BF16), pltpu.VMEM(dirichlet_factor.shape[1:], BF16),
        pltpu.VMEM(face_block.shape[1:], BF16), pltpu.VMEM(neumann_factor.shape[1:], BF16),
        pltpu.VMEM(primal_basis.shape[1:], BF16), pltpu.VMEM(primal_basis.shape[1:], F32),
        pltpu.VMEM(coarse_matrix.shape[1:], F32), pltpu.VMEM(coarse_block_inverse.shape[1:], F32),
        block(n_grp * WINDOW),
        pltpu.VMEM((loads, width), F32),
        pltpu.VMEM((2 * loads, width), F32), pltpu.VMEM((2 * loads, width), F32),
        block(2), block(2), block(2), block(2), pltpu.VMEM((2, 1, width), F32), pltpu.VMEM((2, 1, width), F32),
        block(2), pltpu.VMEM((loads, width), F32),
        pltpu.VMEM((n_grp, 1, loads), F32), pltpu.VMEM((n_sub, 1, loads), F32),
        pltpu.VMEM((n_grp, 1, loads), F32), pltpu.VMEM((n_sub, 1, loads), F32),
        pltpu.VMEM((loads, width), F32), pltpu.VMEM((loads, width), F32),
        pltpu.SemaphoreType.DMA((40,)),
        pltpu.SemaphoreType.DMA((copies,)), pltpu.SemaphoreType.DMA((copies,)),
    ]
    field = jax.ShapeDtypeStruct(solution.shape, F32)
    outs = pl.pallas_call(
        functools.partial(kernel, n_sub, n_grp),
        out_shape=(field, field, field, jax.ShapeDtypeStruct((1, loads), F32)),
        in_specs=[hbm, hbm, hbm, vmem, smem, hbm, hbm, hbm, hbm, vmem, hbm, hbm, hbm, smem],
        out_specs=(free, free, free, vmem),
        scratch_shapes=scratch,
        compiler_params=pltpu.CompilerParams(
            collective_id=0, has_side_effects=True, vmem_limit_bytes=62 * 1024 * 1024
        ),
    )(
        solution, residual, direction, residual_product.reshape(1, -1), neighbor_slots,
        coupling, dirichlet_factor, face_block, neumann_factor, primal_block, primal_basis,
        coarse_matrix, coarse_block_inverse, coarse_pattern,
    )
    return outs[0], outs[1], outs[2], outs[3].reshape(-1)


def solution(mesh):
    rows = P(("sub", "grp"))
    in_specs = (rows, rows, rows, P()) + (rows,) * 10
    out_specs = (rows, rows, rows, P())
    return jax.shard_map(shards, mesh=mesh, in_specs=in_specs, out_specs=out_specs, check_vma=False)
```

profile of v0, /device:TPU:0, one launch (start us, length us, event | category | flops | bytes accessed | tf_op | source)
XLA Modules:
  0.0 97.1 jit_solution(6208284556872000532)
XLA Ops:
  0.6 89.1 %shard_map.165 = (f32[1,128,2048]{2,1,0:T(8,128)}, f32[1,128,2048]{2,1,0:T(8,128)}, f32[1,128,2048]{2,1,0:T(8,128)}, f32[1,128]{1,0:T(1,128)}) custom-call(f32[1,128,2048]{2,1,0:T(8,128)} %sol_h.1, f32[1,128,2048]{2,1,0:T(8,128)} %res_h.1, f32[1,128,2048]{2,1,0:T(8,128)} %dir_h.1, f32[1,128]{1,0:T(1,128)} %bitcast.2, s32[1,4]{1,0:T(1,128)} %slots.1, ...), custom_call_target="tpu_custom_call" | custom-call | tf_op jit(solution)/shard_map/pallas_call | solution.py:458
  89.7 0.0 copy-start
  89.7 2.3 %copy.22 = f32[1,128,2048]{2,1,0:T(8,128)} copy(f32[1,128,2048]{2,1,0:T(8,128)} %get-tuple-element.16) | data formatting | bytes 2097152
  92.0 2.3 %copy.23 = f32[1,128,2048]{2,1,0:T(8,128)} copy(f32[1,128,2048]{2,1,0:T(8,128)} %get-tuple-element.17) | data formatting | bytes 2097152
  94.3 2.3 %copy.24 = f32[1,128,2048]{2,1,0:T(8,128)} copy(f32[1,128,2048]{2,1,0:T(8,128)} %get-tuple-element.18) | data formatting | bytes 2097152
  96.6 0.0 copy-done
  96.6 0.5 copy.25
Async XLA Ops:
  89.7 6.9 %copy-start = (f32[1,128]{1,0:T(1,128)S(1)}, f32[1,128]{1,0:T(1,128)}, u32[]{:S(2)}) copy-start(f32[1,128]{1,0:T(1,128)} %get-tuple-element.11) | copy-start | bytes 1540
where the time goes:
time: 97.4 us; the launch traced here: 97.1 us
  Pallas kernels  89.1 us (91%)
  local copies, waits for them, and re-layouts  7.4 us (8%)
    pallas_call x1, Pallas kernels, shards(): pl.pallas_call(functools.partial(kernel, n_sub, n_grp), out_shape=(field,...  89.1 us
    unnamed x6, local copies, waits for them, and re-layouts  7.4 us

commit v1 on v0

v1 whole, which is shorter than its diff:
```python
import functools

import jax
import jax.numpy as jnp
from jax import lax
from jax.experimental import pallas as pl
from jax.experimental.pallas import tpu as pltpu
from jax.sharding import PartitionSpec as P

REACH = 2
WINDOW = 2 * REACH + 1
MESH = pl.DeviceIdType.MESH
F32 = jnp.float32
BF16 = jnp.bfloat16
NN = (((1,), (0,)), ((), ()))
NT = (((1,), (1,)), ((), ()))


def split(value):
    high = value.astype(BF16)
    low = (value - high.astype(F32)).astype(BF16)
    return jnp.concatenate([high, low], 1)


def twice(value, axis):
    return jnp.concatenate([value, value], axis)


def dot(lhs, rhs, dims=NN):
    return lax.dot_general(lhs, rhs, dims, preferred_element_type=F32)


def exact(lhs, rhs):
    return lax.dot_general(
        lhs, rhs, NN, preferred_element_type=F32, precision=lax.Precision.HIGHEST
    )


def row_sums(value):
    return jnp.sum(value.T, axis=0, keepdims=True)


def as_columns(row, width):
    return jnp.broadcast_to(row, (width, row.shape[1])).T


def kernel(
    n_sub, n_grp,
    sol_h, res_h, dir_h, rp_ref, slots, coup_h, diri_h, face_h, neum_h, pb_ref, basis_h,
    cmat_h, cinv_h, pattern,
    osol, ores, odir, oprod,
    inv_s, U, R, Uhl, V, A, T, B, Y, RY, Hhl, LS, Ss, Sr, So, ST, Cw, Fd, Fb, Nf, basis,
    cmat, cinv, Wn, acc, crn, rcr, rel, Bs, RB, RC, corr, red_g, red_s, red_g2, red_s2, crs,
    stepb, csem, snd, rcv,
):
    ms = lax.axis_index("sub")
    mg = lax.axis_index("grp")
    width = basis.shape[0]
    nb = Fb.shape[0]
    fb = nb // 4
    n_q = Cw.shape[0] // nb
    counter = [0]
    pending = []

    def sub_at(offset):
        return (lax.rem(ms + offset + n_sub, n_sub), mg)

    def grp_at(offset):
        return (ms, lax.rem(mg + offset + n_grp, n_grp))

    def send(src, dst, device):
        i = counter[0]
        counter[0] += 1
        copy = pltpu.make_async_remote_copy(
            src_ref=src, dst_ref=dst, send_sem=snd.at[i], recv_sem=rcv.at[i],
            device_id=device, device_id_type=MESH,
        )
        copy.start()
        pending.append(copy)
        return copy

    def blocks(ref, d, count=fb, first=0):
        return ref.at[pl.ds(d * fb + first, count)]

    def columns(ref, half, k):
        return ref.at[0, :, pl.ds((half * fb + k) * width, width)]

    def fetch_face(hbm, half, buf, d, sem):
        for k in range(fb):
            pltpu.make_async_copy(columns(hbm, half, k), buf.at[d * fb + k], csem.at[sem]).start()

    def wait_face(buf, d, sem):
        pltpu.make_async_copy(blocks(buf, d), blocks(buf, d), csem.at[sem]).wait()

    fetch_face(dir_h, 0, U, 1, 0)
    fetch_face(dir_h, 1, U, 3, 1)
    neum_copy = pltpu.make_async_copy(neum_h.at[0], Nf, csem.at[7])
    neum_copy.start()

    barrier = pltpu.get_barrier_semaphore()
    for o in range(1, n_sub):
        pl.semaphore_signal(barrier, inc=1, device_id=sub_at(o), device_id_type=MESH)
    for o in range(1, n_grp):
        pl.semaphore_signal(barrier, inc=1, device_id=grp_at(o), device_id_type=MESH)
    weight_copies = [
        pltpu.make_async_copy(face_h.at[0], Fb, csem.at[10]),
        pltpu.make_async_copy(coup_h.at[0], Cw, csem.at[11]),
        pltpu.make_async_copy(diri_h.at[0], Fd, csem.at[12]),
    ]
    for c in weight_copies:
        c.start()
    small = [
        pltpu.make_async_copy(basis_h.at[0], basis, csem.at[4]),
        pltpu.make_async_copy(cmat_h.at[0], cmat, csem.at[5]),
        pltpu.make_async_copy(cinv_h.at[0], cinv, csem.at[6]),
    ]
    for c in small:
        c.start()
    fetch_face(res_h, 0, R, 0, 2)
    fetch_face(res_h, 1, R, 1, 3)
    fetch_face(sol_h, 0, osol, 0, 8)
    fetch_face(sol_h, 1, osol, 1, 9)

    for s in range(4):
        at = jnp.int32(0)
        for d in range(4):
            at = jnp.where(slots[0, d] == s, jnp.int32(d * fb), at)
        inv_s[s] = at
    acc[...] = jnp.zeros_like(acc)
    row = lax.broadcasted_iota(jnp.int32, (width, width), 0)
    col = lax.broadcasted_iota(jnp.int32, (width, width), 1)

    def prepare(d):
        def body(k, carry):
            Uhl[d * fb + k] = split(U[d * fb + k])
            return carry
        lax.fori_loop(0, fb, body, 0, unroll=2)

    wait_face(U, 1, 0)
    prepare(1)
    wait_face(U, 3, 1)
    prepare(3)

    neum_copy.wait()
    pairs_n = fb // 2

    def gram(d, k):
        factor = Nf[slots[0, d] * fb + k]
        return dot(factor, factor, NT)

    for side in range(2):
        def own(k, carry, side=side):
            So[side * fb + k] = gram(2 * side + 1, k)
            return carry
        lax.fori_loop(0, fb, own, 0, unroll=4)

        def other(k, carry, side=side):
            first = gram(2 * side, k)
            second = gram(2 * side, k + pairs_n)
            Ss[side, k] = jnp.where(row <= col, first, second)
            diagonal = jnp.sum(jnp.where(row == col, second, 0.0), axis=0, keepdims=True)
            Ss[side, pairs_n, pl.ds(8 * k, 8)] = jnp.broadcast_to(diagonal, (8, width))
            return carry
        lax.fori_loop(0, pairs_n, other, 0, unroll=2)

    small[0].wait()
    basis32 = basis[...].astype(F32)
    primal = pb_ref[...].astype(F32)
    for side in range(2):
        Bs[side, pl.ds(0, width)] = basis32
        shifted = primal - (slots[0, 2 * side] * fb).astype(F32)
        Bs[side, pl.ds(width, 8)] = jnp.broadcast_to(shifted, (8, width))

    pl.semaphore_wait(barrier, n_sub + n_grp - 2)
    u_sub = send(blocks(U, 1), blocks(U, 0), sub_at(1))
    u_grp = send(blocks(U, 3), blocks(U, 2), grp_at(1))
    for c in weight_copies:
        c.wait()

    inner = [(q, k) for k in range(fb) for q in range(n_q) if k + q + 1 < fb]
    outer = [(q, k) for k in range(fb) for q in range(n_q) if k + q + 1 >= fb]
    halves = 2 if len(inner) % 2 == 0 and fb % 2 == 0 else 1
    count = len(inner) // halves
    faces = fb // halves

    def chains(items, total):
        for i, (left, right, n, _) in enumerate(items):
            weight = Cw[n]
            A[i] = split(dot(
                jnp.concatenate([Uhl[left], Uhl[right]], 1),
                jnp.concatenate([twice(weight[:width], 0), twice(weight[width:], 0)], 0),
            ))
        for i, (_, _, n, _) in enumerate(items):
            t = dot(A[i], twice(Fd[n], 0))
            total = total + t * t
            T[i] = split(t)
        for i, (_, _, n, at) in enumerate(items):
            B[at] = split(dot(T[i], twice(Fd[n], 1), NT))
        return total

    def intra(d, h):
        base = d * fb
        j = slots[0, d] * fb
        total = acc[...]
        for g in range(faces):
            k = h * faces + g
            v = dot(Uhl[base + k], twice(Fb[j + k], 0))
            V[base + k] = v
            total = total + U[base + k] * v
        items = []
        for g in range(count):
            q, k = inner[g]
            if halves == 2:
                q = q + h * (inner[count + g][0] - q)
                k = k + h * (inner[count + g][1] - k)
            items.append((base + k, base + k + q + 1, q * nb + j + k, q * nb + base + k))
        acc[...] = chains(items, total)

    def intra_face(d):
        def body(h, carry):
            intra(d, h)
            return carry
        lax.fori_loop(0, halves, body, 0)

    def cross(rs):
        items = []
        for r in rs:
            s = lax.rem(slots[0, 0] + r, 4)
            left = inv_s[s]
            right = inv_s[lax.rem(s + 1, 4)]
            for q, k in outer:
                items.append((left + k, right + k + q + 1 - fb, q * nb + s * fb + k, q * nb + r * fb + k))
        acc[...] = chains(items, acc[...])

    def own_faces(i, carry):
        intra(1 + 2 * (i // halves), lax.rem(i, halves))
        return carry
    lax.fori_loop(0, 2 * halves, own_faces, 0)

    u_grp.wait_recv()
    prepare(2)
    intra_face(2)

    u_sub.wait_recv()
    b_sub = send(Bs.at[0], RB.at[0], sub_at(-1))
    b_grp = send(Bs.at[1], RB.at[1], grp_at(-1))
    prepare(0)
    intra_face(0)
    cross((3, 0))

    def returned(d, h):
        j = slots[0, d] * fb
        turn = lax.rem(slots[0, d] - slots[0, 0] + 4, 4)
        before = lax.rem(turn + 3, 4)
        for g in range(faces):
            k = h * faces + g
            lhs = []
            rhs = []
            for q in range(n_q):
                near = jnp.where(k + q + 1 < fb, d, turn) * fb + k
                back = k - q - 1
                far = jnp.where(back >= 0, d * fb + back, before * fb + back + fb)
                lhs += [B[q * nb + near], B[q * nb + far]]
                rhs += [
                    twice(Cw[q * nb + j + k, :width], 1),
                    twice(Cw[q * nb + lax.rem(j + back + nb, nb), width:], 1),
                ]
            y = dot(jnp.concatenate(lhs, 1), jnp.concatenate(rhs, 1), NT)
            Y[d * fb + k] = y + V[d * fb + k]

    def returned_face(d):
        def body(h, carry):
            returned(d, h)
            return carry
        lax.fori_loop(0, halves, body, 0)

    y_sub = []
    for h in range(halves):
        returned(0, h)
        y_sub.append(send(blocks(Y, 0, faces, h * faces), blocks(RY, 0, faces, h * faces), sub_at(-1)))

    cross((1, 2))

    def reduce_start(value, red, index, size, at):
        red[index] = value
        return [send(red.at[index], red.at[index], at(o)) for o in range(1, size)]

    def reduce_end(copies, red, size):
        for c in copies:
            c.wait_recv()
        for c in copies:
            c.wait_send()
            pending[:] = [other for other in pending if other is not c]
        total = red[0]
        for i in range(1, size):
            total = total + red[i]
        return total

    copies = reduce_start(row_sums(acc[...]), red_g, mg, n_grp, grp_at)
    returned_face(2)
    y_grp = [send(blocks(Y, 2), blocks(RY, 1), grp_at(-1))]
    s_sub = send(Ss.at[0], Sr.at[0], sub_at(-1))
    s_grp = send(Ss.at[1], Sr.at[1], grp_at(-1))
    part = reduce_end(copies, red_g, n_grp)
    copies = reduce_start(part, red_s, ms, n_sub, sub_at)
    returned_face(1)
    returned_face(3)
    curvature = reduce_end(copies, red_s, n_sub)
    rp = rp_ref[...]
    stepb[...] = as_columns(rp / curvature, width)

    wait_face(osol, 0, 8)
    wait_face(osol, 1, 9)
    for half in range(2):
        def iterate(k, carry, half=half):
            osol[half * fb + k] = osol[half * fb + k] + stepb[...] * U[(2 * half + 1) * fb + k]
            return carry
        lax.fori_loop(0, fb, iterate, 0, unroll=2)

    b_sub.wait_recv()
    b_grp.wait_recv()
    for c in small[1:3]:
        c.wait()
    wait_face(R, 0, 2)
    wait_face(R, 1, 3)
    for side in range(2):
        rel[side] = as_columns(RB[side, pl.ds(width, 1)], width)
    pbc = as_columns(primal, width)
    acc[...] = jnp.zeros_like(acc)

    def pick(j):
        return jnp.where(pbc == j.astype(F32), basis32, 0.0).astype(BF16)

    def pick_other(side, k):
        return jnp.where(rel[side] == lax.convert_element_type(k, F32), RB[side, pl.ds(0, width)], 0.0).astype(BF16)

    def residual_face(side, arrivals):
        d = 2 * side + 1
        for c in arrivals:
            c.wait_recv()
        lhs = []
        rhs = []
        for k in range(fb):
            i = side * fb + k
            new = R[i] - stepb[...] * (Y[d * fb + k] + RY[i])
            ores[i] = new
            Hhl[i] = split(new * 0.5)
            lhs.append(Hhl[i])
            rows = jnp.concatenate([pick(slots[0, d] * fb + k), pick_other(side, k)], 0)
            rhs.append(twice(rows, 1))
        both = dot(jnp.concatenate(lhs, 1), jnp.concatenate(rhs, 1), NT)
        crn[side] = both[:, width:]
        return both[:, :width]

    cr3 = residual_face(1, y_grp)
    cr_grp = send(crn.at[1], rcr.at[1], grp_at(1))
    cr1 = residual_face(0, y_sub)
    cr_sub = send(crn.at[0], rcr.at[0], sub_at(1))
    crs[...] = cr1 + cr3

    s_grp.wait_recv()
    s_sub.wait_recv()

    def join(side):
        def body(k, carry):
            packed = Sr[side, k]
            turned = packed.T
            diagonal = Sr[side, pairs_n, pl.ds(8 * k, 1)]
            first = jnp.where(row <= col, packed, turned)
            second = jnp.where(row > col, packed, jnp.where(row < col, turned, diagonal))
            ST[side * fb + k] = split(So[side * fb + k] + first)
            ST[side * fb + k + pairs_n] = split(So[side * fb + k + pairs_n] + second)
            return carry
        lax.fori_loop(0, pairs_n, body, 0, unroll=2)

    def local_face(side):
        def body(k, carry):
            i = side * fb + k
            hl = Hhl[i]
            both = ST[i]
            high = both[:, :width]
            solved = dot(
                jnp.concatenate([hl, hl[:, :width]], 1),
                jnp.concatenate([high, high, both[:, width:]], 0),
            )
            LS[i] = 0.5 * solved
            acc[...] += (0.5 * ores[i]) * solved
            return carry
        lax.fori_loop(0, fb, body, 0, unroll=4)

    join(1)
    join(0)
    cr_grp.wait_recv()
    cr_sub.wait_recv()
    cr = crs[...] + rcr[0] + rcr[1]
    crs[...] = cr
    first = exact(cr, cinv[...])

    def place(g, p):
        return Wn.at[g * WINDOW + p]

    Wn[mg * WINDOW + REACH] = first
    arrivals = {}
    for o in (1, -1, 2, -2):
        p = REACH - o
        arrivals[p] = send(place(mg, REACH), place(mg, p), sub_at(o))
    order = (REACH, REACH - 2, REACH + 2, REACH - 1, REACH + 1)
    column_copies = []
    if n_grp == 4:
        near = (ms, mg + 1 - 2 * lax.rem(mg, 2))
        far = lax.rem(mg + 2, 4)
        far_copies = {}

        def pass_on(p):
            far_copies[p] = send(place(mg, p), place(mg, p), (ms, far))
            column_copies.append(send(place(mg, p), place(mg, p), near))
        pass_on(REACH)
        local_face(1)
        local_face(0)
        for p in order[1:]:
            arrivals[p].wait_recv()
            pass_on(p)
        for p in order:
            far_copies[p].wait_recv()
            column_copies.append(send(place(far, p), place(far, p), near))
        for c in column_copies:
            c.wait_recv()
    else:
        local_face(1)
        local_face(0)
        for p in order:
            if p != REACH:
                arrivals[p].wait_recv()
            for o in range(1, n_grp):
                column_copies.append(send(place(mg, p), place(mg, p), grp_at(o)))
        for c in column_copies:
            c.wait_recv()

    chosen = []
    for k in range(cmat.shape[0]):
        entry = pattern[0, k]
        p = lax.min(lax.rem(entry // n_grp - ms + REACH + n_sub, n_sub), jnp.int32(WINDOW - 1))
        chosen.append(Wn[lax.rem(entry, n_grp) * WINDOW + p])
    adjacent = exact(
        jnp.concatenate(chosen, 1), cmat[...].reshape(cmat.shape[0] * width, width)
    )
    correction = Wn[mg * WINDOW + REACH] + exact(crs[...] - adjacent, cinv[...])
    corr[...] = correction
    c_sub = send(corr, RC.at[0], sub_at(-1))
    c_grp = send(corr, RC.at[1], grp_at(-1))
    product_row = row_sums(acc[...] + correction * crs[...])
    copies = reduce_start(product_row, red_g2, mg, n_grp, grp_at)

    corr_hl = split(correction * 0.5)

    def own_spread(side):
        def body(k, carry):
            i = side * fb + k
            rows = pick(slots[0, 2 * side + 1] * fb + k)
            LS[i] = LS[i] + dot(corr_hl, twice(rows, 0))
            return carry
        lax.fori_loop(0, fb, body, 0, unroll=4)

    own_spread(0)
    part = reduce_end(copies, red_g2, n_grp)
    copies = reduce_start(part, red_s2, ms, n_sub, sub_at)
    own_spread(1)

    def borrowed_spread(side):
        other_hl = split(RC[side] * 0.5)

        def body(k, carry):
            i = side * fb + k
            rows = pick_other(side, k)
            LS[i] = LS[i] + dot(other_hl, twice(rows, 0))
            return carry
        lax.fori_loop(0, fb, body, 0, unroll=4)

    c_grp.wait_recv()
    borrowed_spread(1)
    c_sub.wait_recv()
    borrowed_spread(0)
    product = reduce_end(copies, red_s2, n_sub)
    oprod[...] = product
    ratio = as_columns(product / rp, width)
    for half in range(2):
        def advance(k, carry, half=half):
            odir[half * fb + k] = LS[half * fb + k] + ratio * U[(2 * half + 1) * fb + k]
            return carry
        lax.fori_loop(0, fb, advance, 0, unroll=2)
    for c in pending:
        c.wait_send()


def store(sol, res, dirn, prod, osol, ores, odir, oprod, sem):
    width = sol.shape[2]
    for n, (src, dst) in enumerate(((sol, osol), (res, ores), (dirn, odir))):
        for i in range(src.shape[0]):
            pltpu.make_async_copy(src.at[i], dst.at[0, :, pl.ds(i * width, width)], sem.at[n]).start()
    oprod[...] = prod[...].reshape(oprod.shape)
    for n, src in enumerate((sol, res, dirn)):
        pltpu.make_async_copy(src, src, sem.at[n]).wait()


def shards(
    solution, residual, direction, residual_product, neighbor_slots, coupling,
    dirichlet_factor, face_block, neumann_factor, primal_block, primal_basis,
    coarse_matrix, coarse_block_inverse, coarse_pattern,
):
    n_sub = lax.axis_size("sub")
    n_grp = lax.axis_size("grp")
    loads = direction.shape[1]
    nb = face_block.shape[1]
    width = face_block.shape[2]
    fb = nb // 4
    inner = coupling.shape[1]
    copies = 8 + 4 + 2 + 2 + 4 + 3 * WINDOW + 2 * (n_sub + n_grp) + WINDOW * n_grp
    hbm = pl.BlockSpec(memory_space=pltpu.HBM)
    free = pl.BlockSpec(memory_space=pl.ANY)
    vmem = pl.BlockSpec(memory_space=pltpu.VMEM)
    smem = pl.BlockSpec(memory_space=pltpu.SMEM)

    def block(count, dtype=F32, cols=width):
        return pltpu.VMEM((count, loads, cols), dtype)

    group = 2 * inner // nb * (inner // nb + 1)
    group = max(group, fb * (inner // nb))
    packed = (2, fb // 2 + 1, width, width)
    scratch = [
        pltpu.SMEM((4,), jnp.int32),
        block(nb), block(2 * fb), block(nb, BF16, 2 * width), block(nb),
        block(group, BF16, 2 * width), block(group, BF16, 2 * width),
        block(inner, BF16, 2 * width), block(nb), block(2 * fb),
        block(2 * fb, BF16, 2 * width), block(2 * fb),
        pltpu.VMEM(packed, F32), pltpu.VMEM(packed, F32),
        pltpu.VMEM((2 * fb, width, width), F32), pltpu.VMEM((2 * fb, width, 2 * width), BF16),
        pltpu.VMEM(coupling.shape[1:], BF16), pltpu.VMEM(dirichlet_factor.shape[1:], BF16),
        pltpu.VMEM(face_block.shape[1:], BF16), pltpu.VMEM(neumann_factor.shape[1:], BF16),
        pltpu.VMEM(primal_basis.shape[1:], BF16),
        pltpu.VMEM(coarse_matrix.shape[1:], F32), pltpu.VMEM(coarse_block_inverse.shape[1:], F32),
        block(n_grp * WINDOW),
        pltpu.VMEM((loads, width), F32),
        block(2), block(2), block(2),
        pltpu.VMEM((2, width + 8, width), F32), pltpu.VMEM((2, width + 8, width), F32),
        block(2), pltpu.VMEM((loads, width), F32),
        pltpu.VMEM((n_grp, 1, loads), F32), pltpu.VMEM((n_sub, 1, loads), F32),
        pltpu.VMEM((n_grp, 1, loads), F32), pltpu.VMEM((n_sub, 1, loads), F32),
        pltpu.VMEM((loads, width), F32), pltpu.VMEM((loads, width), F32),
        pltpu.SemaphoreType.DMA((16,)),
        pltpu.SemaphoreType.DMA((copies,)), pltpu.SemaphoreType.DMA((copies,)),
    ]
    field = pltpu.VMEM((2 * fb, loads, width), F32)
    kept = pl.pallas_call(
        functools.partial(kernel, n_sub, n_grp),
        out_shape=(field, field, field, pltpu.VMEM((1, loads), F32)),
        in_specs=[hbm, hbm, hbm, vmem, smem, hbm, hbm, hbm, hbm, vmem, hbm, hbm, hbm, smem],
        out_specs=(vmem, vmem, vmem, vmem),
        scratch_shapes=scratch,
        compiler_params=pltpu.CompilerParams(
            collective_id=0, has_side_effects=True, vmem_limit_bytes=56 * 1024 * 1024
        ),
    )(
        solution, residual, direction, residual_product.reshape(1, -1), neighbor_slots,
        coupling, dirichlet_factor, face_block, neumann_factor, primal_block, primal_basis,
        coarse_matrix, coarse_block_inverse, coarse_pattern,
    )
    whole = jax.ShapeDtypeStruct(solution.shape, F32)
    return pl.pallas_call(
        store,
        out_shape=(whole, whole, whole, jax.ShapeDtypeStruct((loads,), F32)),
        in_specs=[vmem, vmem, vmem, vmem],
        out_specs=(free, free, free, vmem),
        scratch_shapes=[pltpu.SemaphoreType.DMA((3,))],
    )(*[pltpu.with_memory_space_constraint(x, pltpu.VMEM) for x in kept])


def solution(mesh):
    rows = P(("sub", "grp"))
    in_specs = (rows, rows, rows, P()) + (rows,) * 10
    out_specs = (rows, rows, rows, P())
    return jax.shard_map(shards, mesh=mesh, in_specs=in_specs, out_specs=out_specs, check_vma=False)
```

time: 97.4 us -> 77.4 us (0.79)
  Pallas kernels: 89.1 us -> 76.6 us
  local copies, waits for them, and re-layouts: 7.4 us -> 0 us
    pallas_call x1, Pallas kernels: 89.1 us -> 74.5 us  [shards(): pl.pallas_call(functools.partial(kernel, n_sub, n_grp), out_shape=(field,...]
    unnamed x6 -> x0, local copies, waits for them, and re-layouts: 7.4 us -> none
    pallas_call x0 -> x1, Pallas kernels: none -> 2.16 us  [shards(): pl.pallas_call(store, out_shape=(whole, whole, whole, jax.ShapeDtypeStruc...]
where the time goes in v1:
time: 77.4 us; the launch traced here: 77.3 us
  Pallas kernels  76.6 us (99%)
    pallas_call x1, Pallas kernels, shards(): pl.pallas_call(functools.partial(kernel, n_sub, n_grp), out_shape=(field,...  74.5 us
    pallas_call x1, Pallas kernels, shards(): pl.pallas_call(store, out_shape=(whole, whole, whole, jax.ShapeDtypeStruc...  2.16 us

profile of v1, /device:TPU:0, one launch (start us, length us, event | category | flops | bytes accessed | tf_op | source)
XLA Modules:
  0.0 77.3 jit_solution(18424944391829121119)
XLA Ops:
  0.6 74.5 %shard_map.165 = (f32[16,128,128]{2,1,0:T(8,128)S(1)}, f32[16,128,128]{2,1,0:T(8,128)S(1)}, f32[16,128,128]{2,1,0:T(8,128)S(1)}, f32[1,128]{1,0:T(1,128)S(1)}) custom-call(f32[1,128,2048]{2,1,0:T(8,128)} %sol_h.1, f32[1,128,2048]{2,1,0:T(8,128)} %res_h.1, f32[1,128,2048]{2,1,0:T(8,128)} %dir_h.1, f32[1,128]{1,0:T(1,128)} %bitcast.1, s32[1,4]{1,0:T(1,128)} %slots.1, ...), custom_call_target="tpu_custom_call" | custom-call | tf_op jit(solution)/shard_map/pallas_call | solution.py:553
  75.1 2.2 %shard_map.166 = (f32[1,128,2048]{2,1,0:T(8,128)}, f32[1,128,2048]{2,1,0:T(8,128)}, f32[1,128,2048]{2,1,0:T(8,128)}, f32[128]{0:T(128)}) custom-call(f32[16,128,128]{2,1,0:T(8,128)S(1)} %get-tuple-element.8.sol, f32[16,128,128]{2,1,0:T(8,128)S(1)} %get-tuple-element.9.res, f32[16,128,128]{2,1,0:T(8,128)S(1)} %get-tuple-element.10.dirn, ...), custom_call_target="tpu_custom_call" | custom-call | tf_op jit(solution)/shard_map/pallas_call | solution.py:568

commit v2 on v1

--- a/solution.py
+++ b/solution.py
@@ -30,10 +30,16 @@
     return lax.dot_general(lhs, rhs, dims, preferred_element_type=F32)
 
 
-def exact(lhs, rhs):
-    return lax.dot_general(
-        lhs, rhs, NN, preferred_element_type=F32, precision=lax.Precision.HIGHEST
-    )
+def weights(value):
+    high = value.astype(BF16)
+    low = (value - high.astype(F32)).astype(BF16)
+    return jnp.concatenate([high, high, low], 0)
+
+
+def fine(value):
+    high = value.astype(BF16)
+    low = (value - high.astype(F32)).astype(BF16)
+    return jnp.concatenate([high, low, high], 1)
 
 
 def row_sums(value):
@@ -46,12 +52,12 @@
 
 def kernel(
     n_sub, n_grp,
-    sol_h, res_h, dir_h, rp_ref, slots, coup_h, diri_h, face_h, neum_h, pb_ref, basis_h,
-    cmat_h, cinv_h, pattern,
+    sol_h, res_h, dir_h, rp_h, slots_h, coup_h, diri_h, face_h, neum_h, pb_h, basis_h,
+    cmat_h, cinv_h, pattern_h,
     osol, ores, odir, oprod,
-    inv_s, U, R, Uhl, V, A, T, B, Y, RY, Hhl, LS, Ss, Sr, So, ST, Cw, Fd, Fb, Nf, basis,
-    cmat, cinv, Wn, acc, crn, rcr, rel, Bs, RB, RC, corr, red_g, red_s, red_g2, red_s2, crs,
-    stepb, csem, snd, rcv,
+    slots, pattern, inv_s, rp_ref, pb_ref, U, R, Uhl, V, A, T, B, Y, RY, Hhl, LS, Ss, Sr, So, ST,
+    Cw, Fd, Fb, Nf, basis, cmat, cinv, cmat3, cinv3, Wn, acc, crn, rcr, rel, Bs, RB, RC, corr,
+    PK, PO, red_a, red_b, crs, stepb, csem, snd, rcv,
 ):
     ms = lax.axis_index("sub")
     mg = lax.axis_index("grp")
@@ -92,16 +98,33 @@
     def wait_face(buf, d, sem):
         pltpu.make_async_copy(blocks(buf, d), blocks(buf, d), csem.at[sem]).wait()
 
+    barrier = pltpu.get_barrier_semaphore()
+    others = [(i, j) for i in range(n_sub) for j in range(n_grp) if i + j > 0]
+
+    def device_at(i, j):
+        return (lax.rem(ms + i, n_sub), lax.rem(mg + j, n_grp))
+
+    tiny = [
+        pltpu.make_async_copy(slots_h, slots, csem.at[13]),
+        pltpu.make_async_copy(pattern_h, pattern, csem.at[14]),
+        pltpu.make_async_copy(rp_h, rp_ref, csem.at[15]),
+        pltpu.make_async_copy(pb_h, pb_ref, csem.at[16]),
+    ]
     fetch_face(dir_h, 0, U, 1, 0)
     fetch_face(dir_h, 1, U, 3, 1)
+    for i, j in others:
+        pl.semaphore_signal(barrier, inc=1, device_id=device_at(i, j), device_id_type=MESH)
+    tiny[0].start()
     neum_copy = pltpu.make_async_copy(neum_h.at[0], Nf, csem.at[7])
+    small = [
+        pltpu.make_async_copy(basis_h.at[0], basis, csem.at[4]),
+        pltpu.make_async_copy(cmat_h.at[0], cmat, csem.at[5]),
+        pltpu.make_async_copy(cinv_h.at[0], cinv, csem.at[6]),
+    ]
     neum_copy.start()
-
-    barrier = pltpu.get_barrier_semaphore()
-    for o in range(1, n_sub):
-        pl.semaphore_signal(barrier, inc=1, device_id=sub_at(o), device_id_type=MESH)
-    for o in range(1, n_grp):
-        pl.semaphore_signal(barrier, inc=1, device_id=grp_at(o), device_id_type=MESH)
+    for c in tiny[1:]:
+        c.start()
+    small[0].start()
     weight_copies = [
         pltpu.make_async_copy(face_h.at[0], Fb, csem.at[10]),
         pltpu.make_async_copy(coup_h.at[0], Cw, csem.at[11]),
@@ -109,59 +132,37 @@
     ]
     for c in weight_copies:
         c.start()
-    small = [
-        pltpu.make_async_copy(basis_h.at[0], basis, csem.at[4]),
-        pltpu.make_async_copy(cmat_h.at[0], cmat, csem.at[5]),
-        pltpu.make_async_copy(cinv_h.at[0], cinv, csem.at[6]),
-    ]
-    for c in small:
+    for c in small[1:]:
         c.start()
     fetch_face(res_h, 0, R, 0, 2)
     fetch_face(res_h, 1, R, 1, 3)
     fetch_face(sol_h, 0, osol, 0, 8)
     fetch_face(sol_h, 1, osol, 1, 9)
 
+    wait_face(U, 1, 0)
+    wait_face(U, 3, 1)
+    pl.semaphore_wait(barrier, len(others))
+    u_sub = send(blocks(U, 1), blocks(U, 0), sub_at(1))
+    u_grp = send(blocks(U, 3), blocks(U, 2), grp_at(1))
+
+    def prepare(d):
+        def body(k, carry):
+            Uhl[d * fb + k] = split(U[d * fb + k])
+            return carry
+        lax.fori_loop(0, fb, body, 0, unroll=2)
+
+    prepare(1)
+    prepare(3)
+    acc[...] = jnp.zeros_like(acc)
+    row = lax.broadcasted_iota(jnp.int32, (width, width), 0)
+    col = lax.broadcasted_iota(jnp.int32, (width, width), 1)
+    for c in tiny:
+        c.wait()
     for s in range(4):
         at = jnp.int32(0)
         for d in range(4):
             at = jnp.where(slots[0, d] == s, jnp.int32(d * fb), at)
         inv_s[s] = at
-    acc[...] = jnp.zeros_like(acc)
-    row = lax.broadcasted_iota(jnp.int32, (width, width), 0)
-    col = lax.broadcasted_iota(jnp.int32, (width, width), 1)
-
-    def prepare(d):
-        def body(k, carry):
-            Uhl[d * fb + k] = split(U[d * fb + k])
-            return carry
-        lax.fori_loop(0, fb, body, 0, unroll=2)
-
-    wait_face(U, 1, 0)
-    prepare(1)
-    wait_face(U, 3, 1)
-    prepare(3)
-
-    neum_copy.wait()
-    pairs_n = fb // 2
-
-    def gram(d, k):
-        factor = Nf[slots[0, d] * fb + k]
-        return dot(factor, factor, NT)
-
-    for side in range(2):
-        def own(k, carry, side=side):
-            So[side * fb + k] = gram(2 * side + 1, k)
-            return carry
-        lax.fori_loop(0, fb, own, 0, unroll=4)
-
-        def other(k, carry, side=side):
-            first = gram(2 * side, k)
-            second = gram(2 * side, k + pairs_n)
-            Ss[side, k] = jnp.where(row <= col, first, second)
-            diagonal = jnp.sum(jnp.where(row == col, second, 0.0), axis=0, keepdims=True)
-            Ss[side, pairs_n, pl.ds(8 * k, 8)] = jnp.broadcast_to(diagonal, (8, width))
-            return carry
-        lax.fori_loop(0, pairs_n, other, 0, unroll=2)
 
     small[0].wait()
     basis32 = basis[...].astype(F32)
@@ -171,9 +172,22 @@
         shifted = primal - (slots[0, 2 * side] * fb).astype(F32)
         Bs[side, pl.ds(width, 8)] = jnp.broadcast_to(shifted, (8, width))
 
-    pl.semaphore_wait(barrier, n_sub + n_grp - 2)
-    u_sub = send(blocks(U, 1), blocks(U, 0), sub_at(1))
-    u_grp = send(blocks(U, 3), blocks(U, 2), grp_at(1))
+    neum_copy.wait()
+    pairs_n = fb // 2
+
+    def gram(d, k):
+        factor = Nf[slots[0, d] * fb + k]
+        return dot(factor, factor, NT)
+
+    for side in range(2):
+        def other(k, carry, side=side):
+            first = gram(2 * side, k)
+            second = gram(2 * side, k + pairs_n)
+            Ss[side, k] = jnp.where(row <= col, first, second)
+            diagonal = jnp.sum(jnp.where(row == col, second, 0.0), axis=0, keepdims=True)
+            Ss[side, pairs_n, pl.ds(8 * k, 8)] = jnp.broadcast_to(diagonal, (8, width))
+            return carry
+        lax.fori_loop(0, pairs_n, other, 0, unroll=4)
     for c in weight_copies:
         c.wait()
 
@@ -241,12 +255,53 @@
     prepare(2)
     intra_face(2)
 
-    u_sub.wait_recv()
+    for side in range(2):
+        def own(k, carry, side=side):
+            So[side * fb + k] = gram(2 * side + 1, k)
+            return carry
+        lax.fori_loop(0, fb, own, 0, unroll=4)
+    pbc = as_columns(primal, width)
+    for side in range(2):
+        def keep(k, carry, side=side):
+            j = slots[0, 2 * side + 1] * fb + k
+            PK[side * fb + k] = jnp.where(pbc == j.astype(F32), basis32, 0.0).astype(BF16)
+            return carry
+        lax.fori_loop(0, fb, keep, 0, unroll=4)
+    for c in small[1:]:
+        c.wait()
+    cinv3[...] = weights(cinv[...])
+
+    def halve(k, carry):
+        cmat3[k] = weights(cmat[k])
+        return carry
+    lax.fori_loop(0, cmat.shape[0], halve, 0)
+
+    for c in (u_grp, u_sub):
+        c.wait_send()
+        pending[:] = [other for other in pending if other is not c]
     b_sub = send(Bs.at[0], RB.at[0], sub_at(-1))
     b_grp = send(Bs.at[1], RB.at[1], grp_at(-1))
+    u_sub.wait_recv()
     prepare(0)
     intra_face(0)
-    cross((3, 0))
+
+    def all_cross(i, carry):
+        cross((lax.rem(3 + 2 * i, 4), 2 * i))
+        return carry
+    lax.fori_loop(0, 2, all_cross, 0)
+
+    me = ms * n_grp + mg
+
+    def total_start(value, red):
+        red[me] = value
+        return [send(red.at[me], red.at[me], device_at(i, j)) for i, j in others]
+
+    def total_end(copies, red):
+        for c in copies:
+            c.wait_recv()
+        return jnp.sum(red[...], axis=0)
+
+    copies = total_start(row_sums(acc[...]), red_a)
 
     def returned(d, h):
         j = slots[0, d] * fb
@@ -278,37 +333,53 @@
     for h in range(halves):
         returned(0, h)
         y_sub.append(send(blocks(Y, 0, faces, h * faces), blocks(RY, 0, faces, h * faces), sub_at(-1)))
-
-    cross((1, 2))
-
-    def reduce_start(value, red, index, size, at):
-        red[index] = value
-        return [send(red.at[index], red.at[index], at(o)) for o in range(1, size)]
-
-    def reduce_end(copies, red, size):
-        for c in copies:
-            c.wait_recv()
-        for c in copies:
-            c.wait_send()
-            pending[:] = [other for other in pending if other is not c]
-        total = red[0]
-        for i in range(1, size):
-            total = total + red[i]
-        return total
-
-    copies = reduce_start(row_sums(acc[...]), red_g, mg, n_grp, grp_at)
     returned_face(2)
     y_grp = [send(blocks(Y, 2), blocks(RY, 1), grp_at(-1))]
-    s_sub = send(Ss.at[0], Sr.at[0], sub_at(-1))
-    s_grp = send(Ss.at[1], Sr.at[1], grp_at(-1))
-    part = reduce_end(copies, red_g, n_grp)
-    copies = reduce_start(part, red_s, ms, n_sub, sub_at)
     returned_face(1)
+    b_sub.wait_recv()
+    b_grp.wait_recv()
+    for side in range(2):
+        rel[side] = as_columns(RB[side, pl.ds(width, 1)], width)
+
+        def keep_other(k, carry, side=side):
+            rows = jnp.where(rel[side] == k.astype(F32), RB[side, pl.ds(0, width)], 0.0)
+            PO[side * fb + k] = rows.astype(BF16)
+            return carry
+        lax.fori_loop(0, fb, keep_other, 0, unroll=4)
+    wait_face(R, 0, 2)
+    wait_face(R, 1, 3)
+
     returned_face(3)
-    curvature = reduce_end(copies, red_s, n_sub)
+    curvature = total_end(copies, red_a)
     rp = rp_ref[...]
     stepb[...] = as_columns(rp / curvature, width)
 
+    def lend(side):
+        lhs = []
+        rhs = []
+        for k in range(fb):
+            i = side * fb + k
+            part = R[i] - stepb[...] * Y[(2 * side + 1) * fb + k]
+            R[i] = part
+            lhs.append(split(part * 0.5))
+            rhs.append(twice(PO[i], 1))
+        crn[side] = dot(jnp.concatenate(lhs, 1), jnp.concatenate(rhs, 1), NT)
+
+    lend(0)
+    cr_sub = send(crn.at[0], rcr.at[0], sub_at(1))
+    lend(1)
+    cr_grp = send(crn.at[1], rcr.at[1], grp_at(1))
+    s_grp = send(Ss.at[1], Sr.at[1], grp_at(-1))
+
+    lhs = []
+    rhs = []
+    for d in (0, 2):
+        for k in range(fb):
+            j = slots[0, d] * fb + k
+            rows = jnp.where(pbc == j.astype(F32), basis32, 0.0).astype(BF16)
+            lhs.append(split(Y[d * fb + k] * 0.5))
+            rhs.append(twice(rows, 1))
+    crs[...] = -stepb[...] * dot(jnp.concatenate(lhs, 1), jnp.concatenate(rhs, 1), NT)
     wait_face(osol, 0, 8)
     wait_face(osol, 1, 9)
     for half in range(2):
@@ -316,62 +387,21 @@
             osol[half * fb + k] = osol[half * fb + k] + stepb[...] * U[(2 * half + 1) * fb + k]
             return carry
         lax.fori_loop(0, fb, iterate, 0, unroll=2)
-
-    b_sub.wait_recv()
-    b_grp.wait_recv()
-    for c in small[1:3]:
-        c.wait()
-    wait_face(R, 0, 2)
-    wait_face(R, 1, 3)
-    for side in range(2):
-        rel[side] = as_columns(RB[side, pl.ds(width, 1)], width)
-    pbc = as_columns(primal, width)
     acc[...] = jnp.zeros_like(acc)
 
-    def pick(j):
-        return jnp.where(pbc == j.astype(F32), basis32, 0.0).astype(BF16)
-
-    def pick_other(side, k):
-        return jnp.where(rel[side] == lax.convert_element_type(k, F32), RB[side, pl.ds(0, width)], 0.0).astype(BF16)
-
     def residual_face(side, arrivals):
-        d = 2 * side + 1
         for c in arrivals:
             c.wait_recv()
         lhs = []
         rhs = []
         for k in range(fb):
             i = side * fb + k
-            new = R[i] - stepb[...] * (Y[d * fb + k] + RY[i])
+            new = R[i] - stepb[...] * RY[i]
             ores[i] = new
             Hhl[i] = split(new * 0.5)
             lhs.append(Hhl[i])
-            rows = jnp.concatenate([pick(slots[0, d] * fb + k), pick_other(side, k)], 0)
-            rhs.append(twice(rows, 1))
-        both = dot(jnp.concatenate(lhs, 1), jnp.concatenate(rhs, 1), NT)
-        crn[side] = both[:, width:]
-        return both[:, :width]
-
-    cr3 = residual_face(1, y_grp)
-    cr_grp = send(crn.at[1], rcr.at[1], grp_at(1))
-    cr1 = residual_face(0, y_sub)
-    cr_sub = send(crn.at[0], rcr.at[0], sub_at(1))
-    crs[...] = cr1 + cr3
-
-    s_grp.wait_recv()
-    s_sub.wait_recv()
-
-    def join(side):
-        def body(k, carry):
-            packed = Sr[side, k]
-            turned = packed.T
-            diagonal = Sr[side, pairs_n, pl.ds(8 * k, 1)]
-            first = jnp.where(row <= col, packed, turned)
-            second = jnp.where(row > col, packed, jnp.where(row < col, turned, diagonal))
-            ST[side * fb + k] = split(So[side * fb + k] + first)
-            ST[side * fb + k + pairs_n] = split(So[side * fb + k + pairs_n] + second)
-            return carry
-        lax.fori_loop(0, pairs_n, body, 0, unroll=2)
+            rhs.append(twice(PK[i], 1))
+        return dot(jnp.concatenate(lhs, 1), jnp.concatenate(rhs, 1), NT)
 
     def local_face(side):
         def body(k, carry):
@@ -388,13 +418,29 @@
             return carry
         lax.fori_loop(0, fb, body, 0, unroll=4)
 
-    join(1)
-    join(0)
+    def join_face(side):
+        def join(k, carry):
+            packed = Sr[side, k]
+            turned = packed.T
+            diagonal = Sr[side, pairs_n, pl.ds(8 * k, 1)]
+            first = jnp.where(row <= col, packed, turned)
+            second = jnp.where(row > col, packed, jnp.where(row < col, turned, diagonal))
+            ST[side * fb + k] = split(So[side * fb + k] + first)
+            ST[side * fb + k + pairs_n] = split(So[side * fb + k + pairs_n] + second)
+            return carry
+        lax.fori_loop(0, pairs_n, join, 0, unroll=2)
+
+    crs[...] += residual_face(1, y_grp)
+    s_grp.wait_recv()
+    join_face(1)
+    local_face(1)
     cr_grp.wait_recv()
+    crs[...] += rcr[1]
+    crs[...] += residual_face(0, y_sub)
     cr_sub.wait_recv()
-    cr = crs[...] + rcr[0] + rcr[1]
+    cr = crs[...] + rcr[0]
     crs[...] = cr
-    first = exact(cr, cinv[...])
+    first = dot(fine(cr), cinv3[...])
 
     def place(g, p):
         return Wn.at[g * WINDOW + p]
@@ -415,24 +461,28 @@
             far_copies[p] = send(place(mg, p), place(mg, p), (ms, far))
             column_copies.append(send(place(mg, p), place(mg, p), near))
         pass_on(REACH)
-        local_face(1)
-        local_face(0)
         for p in order[1:]:
             arrivals[p].wait_recv()
             pass_on(p)
+        s_sub = send(Ss.at[0], Sr.at[0], sub_at(-1))
         for p in order:
             far_copies[p].wait_recv()
             column_copies.append(send(place(far, p), place(far, p), near))
+        s_sub.wait_recv()
+        join_face(0)
+        local_face(0)
         for c in column_copies:
             c.wait_recv()
     else:
-        local_face(1)
-        local_face(0)
         for p in order:
             if p != REACH:
                 arrivals[p].wait_recv()
             for o in range(1, n_grp):
                 column_copies.append(send(place(mg, p), place(mg, p), grp_at(o)))
+        s_sub = send(Ss.at[0], Sr.at[0], sub_at(-1))
+        s_sub.wait_recv()
+        join_face(0)
+        local_face(0)
         for c in column_copies:
             c.wait_recv()
 
@@ -441,38 +491,31 @@
         entry = pattern[0, k]
         p = lax.min(lax.rem(entry // n_grp - ms + REACH + n_sub, n_sub), jnp.int32(WINDOW - 1))
         chosen.append(Wn[lax.rem(entry, n_grp) * WINDOW + p])
-    adjacent = exact(
-        jnp.concatenate(chosen, 1), cmat[...].reshape(cmat.shape[0] * width, width)
+    adjacent = dot(
+        jnp.concatenate([fine(c) for c in chosen], 1),
+        cmat3[...].reshape(cmat3.shape[0] * cmat3.shape[1], width),
     )
-    correction = Wn[mg * WINDOW + REACH] + exact(crs[...] - adjacent, cinv[...])
+    correction = Wn[mg * WINDOW + REACH] + dot(fine(crs[...] - adjacent), cinv3[...])
     corr[...] = correction
     c_sub = send(corr, RC.at[0], sub_at(-1))
     c_grp = send(corr, RC.at[1], grp_at(-1))
     product_row = row_sums(acc[...] + correction * crs[...])
-    copies = reduce_start(product_row, red_g2, mg, n_grp, grp_at)
+    copies = total_start(product_row, red_b)
 
     corr_hl = split(correction * 0.5)
-
-    def own_spread(side):
+    for side in range(2):
+        def own_spread(k, carry, side=side):
+            i = side * fb + k
+            LS[i] = LS[i] + dot(corr_hl, twice(PK[i], 0))
+            return carry
+        lax.fori_loop(0, fb, own_spread, 0, unroll=4)
+
+    def borrowed_spread(side):
+        other_hl = split(RC[side] * 0.5)
+
         def body(k, carry):
             i = side * fb + k
-            rows = pick(slots[0, 2 * side + 1] * fb + k)
-            LS[i] = LS[i] + dot(corr_hl, twice(rows, 0))
-            return carry
-        lax.fori_loop(0, fb, body, 0, unroll=4)
-
-    own_spread(0)
-    part = reduce_end(copies, red_g2, n_grp)
-    copies = reduce_start(part, red_s2, ms, n_sub, sub_at)
-    own_spread(1)
-
-    def borrowed_spread(side):
-        other_hl = split(RC[side] * 0.5)
-
-        def body(k, carry):
-            i = side * fb + k
-            rows = pick_other(side, k)
-            LS[i] = LS[i] + dot(other_hl, twice(rows, 0))
+            LS[i] = LS[i] + dot(other_hl, twice(PO[i], 0))
             return carry
         lax.fori_loop(0, fb, body, 0, unroll=4)
 
@@ -480,7 +523,7 @@
     borrowed_spread(1)
     c_sub.wait_recv()
     borrowed_spread(0)
-    product = reduce_end(copies, red_s2, n_sub)
+    product = total_end(copies, red_b)
     oprod[...] = product
     ratio = as_columns(product / rp, width)
     for half in range(2):
@@ -514,20 +557,21 @@
     width = face_block.shape[2]
     fb = nb // 4
     inner = coupling.shape[1]
-    copies = 8 + 4 + 2 + 2 + 4 + 3 * WINDOW + 2 * (n_sub + n_grp) + WINDOW * n_grp
+    copies = 16 + 3 * WINDOW + 2 * n_sub * n_grp + WINDOW * n_grp
     hbm = pl.BlockSpec(memory_space=pltpu.HBM)
     free = pl.BlockSpec(memory_space=pl.ANY)
     vmem = pl.BlockSpec(memory_space=pltpu.VMEM)
-    smem = pl.BlockSpec(memory_space=pltpu.SMEM)
 
     def block(count, dtype=F32, cols=width):
         return pltpu.VMEM((count, loads, cols), dtype)
 
-    group = 2 * inner // nb * (inner // nb + 1)
-    group = max(group, fb * (inner // nb))
+    n_q = inner // nb
+    group = max(n_q * (n_q + 1), fb * n_q)
     packed = (2, fb // 2 + 1, width, width)
     scratch = [
+        pltpu.SMEM(neighbor_slots.shape, jnp.int32), pltpu.SMEM(coarse_pattern.shape, jnp.int32),
         pltpu.SMEM((4,), jnp.int32),
+        pltpu.VMEM((1, loads), F32), pltpu.VMEM(primal_block.shape, jnp.int32),
         block(nb), block(2 * fb), block(nb, BF16, 2 * width), block(nb),
         block(group, BF16, 2 * width), block(group, BF16, 2 * width),
         block(inner, BF16, 2 * width), block(nb), block(2 * fb),
@@ -538,22 +582,23 @@
         pltpu.VMEM(face_block.shape[1:], BF16), pltpu.VMEM(neumann_factor.shape[1:], BF16),
         pltpu.VMEM(primal_basis.shape[1:], BF16),
         pltpu.VMEM(coarse_matrix.shape[1:], F32), pltpu.VMEM(coarse_block_inverse.shape[1:], F32),
+        pltpu.VMEM((coarse_matrix.shape[1], 3 * width, width), BF16), pltpu.VMEM((3 * width, width), BF16),
         block(n_grp * WINDOW),
         pltpu.VMEM((loads, width), F32),
         block(2), block(2), block(2),
         pltpu.VMEM((2, width + 8, width), F32), pltpu.VMEM((2, width + 8, width), F32),
         block(2), pltpu.VMEM((loads, width), F32),
-        pltpu.VMEM((n_grp, 1, loads), F32), pltpu.VMEM((n_sub, 1, loads), F32),
-        pltpu.VMEM((n_grp, 1, loads), F32), pltpu.VMEM((n_sub, 1, loads), F32),
+        pltpu.VMEM((2 * fb, width, width), BF16), pltpu.VMEM((2 * fb, width, width), BF16),
+        pltpu.VMEM((n_sub * n_grp, 1, loads), F32), pltpu.VMEM((n_sub * n_grp, 1, loads), F32),
         pltpu.VMEM((loads, width), F32), pltpu.VMEM((loads, width), F32),
-        pltpu.SemaphoreType.DMA((16,)),
+        pltpu.SemaphoreType.DMA((20,)),
         pltpu.SemaphoreType.DMA((copies,)), pltpu.SemaphoreType.DMA((copies,)),
     ]
     field = pltpu.VMEM((2 * fb, loads, width), F32)
     kept = pl.pallas_call(
         functools.partial(kernel, n_sub, n_grp),
         out_shape=(field, field, field, pltpu.VMEM((1, loads), F32)),
-        in_specs=[hbm, hbm, hbm, vmem, smem, hbm, hbm, hbm, hbm, vmem, hbm, hbm, hbm, smem],
+        in_specs=[hbm] * 14,
         out_specs=(vmem, vmem, vmem, vmem),
         scratch_shapes=scratch,
         compiler_params=pltpu.CompilerParams(

time: 77.4 us -> 67.3 us (0.87)
  Pallas kernels: 76.6 us -> 66.5 us
    pallas_call x1, Pallas kernels: 74.5 us -> 64.3 us  [shards(): pl.pallas_call(functools.partial(kernel, n_sub, n_grp), out_shape=(field,...]
where the time goes in v2:
time: 67.3 us; the launch traced here: 67.1 us
  Pallas kernels  66.5 us (99%)
    pallas_call x1, Pallas kernels, shards(): pl.pallas_call(functools.partial(kernel, n_sub, n_grp), out_shape=(field,...  64.3 us
    pallas_call x1, Pallas kernels, shards(): pl.pallas_call(store, out_shape=(whole, whole, whole, jax.ShapeDtypeStruc...  2.16 us

profile of v2, /device:TPU:0, one launch (start us, length us, event | category | flops | bytes accessed | tf_op | source)
XLA Modules:
  0.0 67.1 jit_solution(9012285102356898034)
XLA Ops:
  0.6 64.3 %shard_map.165 = (f32[16,128,128]{2,1,0:T(8,128)S(1)}, f32[16,128,128]{2,1,0:T(8,128)S(1)}, f32[16,128,128]{2,1,0:T(8,128)S(1)}, f32[1,128]{1,0:T(1,128)S(1)}) custom-call(f32[1,128,2048]{2,1,0:T(8,128)} %sol_h.1, f32[1,128,2048]{2,1,0:T(8,128)} %res_h.1, f32[1,128,2048]{2,1,0:T(8,128)} %dir_h.1, f32[1,128]{1,0:T(1,128)} %bitcast.1, s32[1,4]{1,0:T(1,128)} %slots_h.1, ...), custom_call_target="tpu_custom_call" | custom-call | tf_op jit(solution)/shard_map/pallas_call | solution.py:598
  65.0 2.2 %shard_map.166 = (f32[1,128,2048]{2,1,0:T(8,128)}, f32[1,128,2048]{2,1,0:T(8,128)}, f32[1,128,2048]{2,1,0:T(8,128)}, f32[128]{0:T(128)}) custom-call(f32[16,128,128]{2,1,0:T(8,128)S(1)} %get-tuple-element.8.sol, f32[16,128,128]{2,1,0:T(8,128)S(1)} %get-tuple-element.9.res, f32[16,128,128]{2,1,0:T(8,128)S(1)} %get-tuple-element.10.dirn, ...), custom_call_target="tpu_custom_call" | custom-call | tf_op jit(solution)/shard_map/pallas_call | solution.py:613

commit v3 on v2

--- a/solution.py
+++ b/solution.py
@@ -142,14 +142,18 @@
     wait_face(U, 1, 0)
     wait_face(U, 3, 1)
     pl.semaphore_wait(barrier, len(others))
-    u_sub = send(blocks(U, 1), blocks(U, 0), sub_at(1))
+    ahead = fb - max(1, fb // 4)
+    u_sub = [
+        send(blocks(U, 1, ahead), blocks(U, 0, ahead), sub_at(1)),
+        send(blocks(U, 1, fb - ahead, ahead), blocks(U, 0, fb - ahead, ahead), sub_at(1)),
+    ]
     u_grp = send(blocks(U, 3), blocks(U, 2), grp_at(1))
 
-    def prepare(d):
+    def prepare(d, first=0, last=fb):
         def body(k, carry):
             Uhl[d * fb + k] = split(U[d * fb + k])
             return carry
-        lax.fori_loop(0, fb, body, 0, unroll=2)
+        lax.fori_loop(first, last, body, 0, unroll=2)
 
     prepare(1)
     prepare(3)
@@ -171,7 +175,6 @@
         Bs[side, pl.ds(0, width)] = basis32
         shifted = primal - (slots[0, 2 * side] * fb).astype(F32)
         Bs[side, pl.ds(width, 8)] = jnp.broadcast_to(shifted, (8, width))
-
     neum_copy.wait()
     pairs_n = fb // 2
 
@@ -185,7 +188,7 @@
             second = gram(2 * side, k + pairs_n)
             Ss[side, k] = jnp.where(row <= col, first, second)
             diagonal = jnp.sum(jnp.where(row == col, second, 0.0), axis=0, keepdims=True)
-            Ss[side, pairs_n, pl.ds(8 * k, 8)] = jnp.broadcast_to(diagonal, (8, width))
+            Bs[side, pl.ds(width + 8 + 8 * k, 8)] = jnp.broadcast_to(diagonal, (8, width))
             return carry
         lax.fori_loop(0, pairs_n, other, 0, unroll=4)
     for c in weight_copies:
@@ -236,15 +239,25 @@
             return carry
         lax.fori_loop(0, halves, body, 0)
 
-    def cross(rs):
-        items = []
-        for r in rs:
-            s = lax.rem(slots[0, 0] + r, 4)
-            left = inv_s[s]
-            right = inv_s[lax.rem(s + 1, 4)]
-            for q, k in outer:
-                items.append((left + k, right + k + q + 1 - fb, q * nb + s * fb + k, q * nb + r * fb + k))
-        acc[...] = chains(items, acc[...])
+    def boundary(r):
+        s = lax.rem(slots[0, 0] + r, 4)
+        left = inv_s[s]
+        right = inv_s[lax.rem(s + 1, 4)]
+        return [
+            (left + k, right + k + q + 1 - fb, q * nb + s * fb + k, q * nb + r * fb + k)
+            for q, k in outer
+        ]
+
+    def arrived(first, last, items):
+        j = slots[0, 0] * fb
+        total = acc[...]
+        for k in range(first, last):
+            v = dot(Uhl[k], twice(Fb[j + k], 0))
+            V[k] = v
+            total = total + U[k] * v
+        within = [(q, k) for q, k in inner if first <= k + q + 1 < last]
+        items = [(k, k + q + 1, q * nb + j + k, q * nb + k) for q, k in within] + items
+        acc[...] = chains(items, total)
 
     def own_faces(i, carry):
         intra(1 + 2 * (i // halves), lax.rem(i, halves))
@@ -276,29 +289,40 @@
         return carry
     lax.fori_loop(0, cmat.shape[0], halve, 0)
 
-    for c in (u_grp, u_sub):
+    acc[...] = chains(boundary(1) + boundary(2), acc[...])
+
+    for c in [u_grp] + u_sub:
         c.wait_send()
         pending[:] = [other for other in pending if other is not c]
     b_sub = send(Bs.at[0], RB.at[0], sub_at(-1))
     b_grp = send(Bs.at[1], RB.at[1], grp_at(-1))
-    u_sub.wait_recv()
-    prepare(0)
-    intra_face(0)
-
-    def all_cross(i, carry):
-        cross((lax.rem(3 + 2 * i, 4), 2 * i))
-        return carry
-    lax.fori_loop(0, 2, all_cross, 0)
+    u_sub[0].wait_recv()
+    prepare(0, 0, ahead)
+    arrived(0, ahead, boundary(3))
+    u_sub[1].wait_recv()
+    prepare(0, ahead, fb)
+    arrived(ahead, fb, boundary(0))
 
     me = ms * n_grp + mg
+
+    def total_copy(rows, device):
+        i = counter[0]
+        return pltpu.make_async_remote_copy(
+            src_ref=rows, dst_ref=rows, send_sem=snd.at[i], recv_sem=rcv.at[i],
+            device_id=device, device_id_type=MESH,
+        )
 
     def total_start(value, red):
         red[me] = value
-        return [send(red.at[me], red.at[me], device_at(i, j)) for i, j in others]
-
-    def total_end(copies, red):
-        for c in copies:
-            c.wait_recv()
+        for i, j in others:
+            total_copy(red.at[me], device_at(i, j)).start()
+        every = total_copy(red.at[pl.ds(0, len(others))], device_at(*others[0]))
+        counter[0] += 1
+        pending.append(every)
+        return every
+
+    def total_end(every, red):
+        every.wait_recv()
         return jnp.sum(red[...], axis=0)
 
     copies = total_start(row_sums(acc[...]), red_a)
@@ -422,7 +446,7 @@
         def join(k, carry):
             packed = Sr[side, k]
             turned = packed.T
-            diagonal = Sr[side, pairs_n, pl.ds(8 * k, 1)]
+            diagonal = RB[side, pl.ds(width + 8 + 8 * k, 1)]
             first = jnp.where(row <= col, packed, turned)
             second = jnp.where(row > col, packed, jnp.where(row < col, turned, diagonal))
             ST[side * fb + k] = split(So[side * fb + k] + first)
@@ -442,14 +466,18 @@
     crs[...] = cr
     first = dot(fine(cr), cinv3[...])
 
-    def place(g, p):
-        return Wn.at[g * WINDOW + p]
+    pieces = 1
+    rows = first.shape[0] // pieces
+
+    def place(g, p, h):
+        return Wn.at[g * WINDOW + p, pl.ds(h * rows, rows)]
 
     Wn[mg * WINDOW + REACH] = first
     arrivals = {}
-    for o in (1, -1, 2, -2):
-        p = REACH - o
-        arrivals[p] = send(place(mg, REACH), place(mg, p), sub_at(o))
+    for h in range(pieces):
+        for o in (2, -2, 1, -1):
+            p = REACH - o
+            arrivals[p, h] = send(place(mg, REACH, h), place(mg, p, h), sub_at(o))
     order = (REACH, REACH - 2, REACH + 2, REACH - 1, REACH + 1)
     column_copies = []
     if n_grp == 4:
@@ -457,17 +485,21 @@
         far = lax.rem(mg + 2, 4)
         far_copies = {}
 
-        def pass_on(p):
-            far_copies[p] = send(place(mg, p), place(mg, p), (ms, far))
-            column_copies.append(send(place(mg, p), place(mg, p), near))
-        pass_on(REACH)
-        for p in order[1:]:
-            arrivals[p].wait_recv()
-            pass_on(p)
-        s_sub = send(Ss.at[0], Sr.at[0], sub_at(-1))
+        def pass_on(p, h):
+            far_copies[p, h] = send(place(mg, p, h), place(mg, p, h), (ms, far))
+            column_copies.append(send(place(mg, p, h), place(mg, p, h), near))
+        for h in range(pieces):
+            pass_on(REACH, h)
+        for i, p in enumerate(order[1:]):
+            for h in range(pieces):
+                arrivals[p, h].wait_recv()
+                pass_on(p, h)
+            if i == 0:
+                s_sub = send(Ss.at[0], Sr.at[0], sub_at(-1))
         for p in order:
-            far_copies[p].wait_recv()
-            column_copies.append(send(place(far, p), place(far, p), near))
+            for h in range(pieces):
+                far_copies[p, h].wait_recv()
+                column_copies.append(send(place(far, p, h), place(far, p, h), near))
         s_sub.wait_recv()
         join_face(0)
         local_face(0)
@@ -475,10 +507,11 @@
             c.wait_recv()
     else:
         for p in order:
-            if p != REACH:
-                arrivals[p].wait_recv()
-            for o in range(1, n_grp):
-                column_copies.append(send(place(mg, p), place(mg, p), grp_at(o)))
+            for h in range(pieces):
+                if p != REACH:
+                    arrivals[p, h].wait_recv()
+                for o in range(1, n_grp):
+                    column_copies.append(send(place(mg, p, h), place(mg, p, h), grp_at(o)))
         s_sub = send(Ss.at[0], Sr.at[0], sub_at(-1))
         s_sub.wait_recv()
         join_face(0)
@@ -557,7 +590,7 @@
     width = face_block.shape[2]
     fb = nb // 4
     inner = coupling.shape[1]
-    copies = 16 + 3 * WINDOW + 2 * n_sub * n_grp + WINDOW * n_grp
+    copies = 16 + 2 * WINDOW + WINDOW * (n_grp - 1)
     hbm = pl.BlockSpec(memory_space=pltpu.HBM)
     free = pl.BlockSpec(memory_space=pl.ANY)
     vmem = pl.BlockSpec(memory_space=pltpu.VMEM)
@@ -567,7 +600,7 @@
 
     n_q = inner // nb
     group = max(n_q * (n_q + 1), fb * n_q)
-    packed = (2, fb // 2 + 1, width, width)
+    packed = (2, fb // 2, width, width)
     scratch = [
         pltpu.SMEM(neighbor_slots.shape, jnp.int32), pltpu.SMEM(coarse_pattern.shape, jnp.int32),
         pltpu.SMEM((4,), jnp.int32),
@@ -586,7 +619,7 @@
         block(n_grp * WINDOW),
         pltpu.VMEM((loads, width), F32),
         block(2), block(2), block(2),
-        pltpu.VMEM((2, width + 8, width), F32), pltpu.VMEM((2, width + 8, width), F32),
+        pltpu.VMEM((2, width + 8 + 4 * fb, width), F32), pltpu.VMEM((2, width + 8 + 4 * fb, width), F32),
         block(2), pltpu.VMEM((loads, width), F32),
         pltpu.VMEM((2 * fb, width, width), BF16), pltpu.VMEM((2 * fb, width, width), BF16),
         pltpu.VMEM((n_sub * n_grp, 1, loads), F32), pltpu.VMEM((n_sub * n_grp, 1, loads), F32),

time: 67.3 us -> 59.9 us (0.89)
  Pallas kernels: 66.5 us -> 59.1 us
    pallas_call x1, Pallas kernels: 64.3 us -> 57 us  [shards(): pl.pallas_call(functools.partial(kernel, n_sub, n_grp), out_shape=(field,...]
where the time goes in v3:
time: 59.9 us; the launch traced here: 59.8 us
  Pallas kernels  59.1 us (99%)
  between operations  0.64 us (1%)
    pallas_call x1, Pallas kernels, shards(): pl.pallas_call(functools.partial(kernel, n_sub, n_grp), out_shape=(field,...  57 us
    pallas_call x1, Pallas kernels, shards(): pl.pallas_call(store, out_shape=(whole, whole, whole, jax.ShapeDtypeStruc...  2.16 us

profile of v3, /device:TPU:0, one launch (start us, length us, event | category | flops | bytes accessed | tf_op | source)
XLA Modules:
  0.0 59.8 jit_solution(11271554181322698454)
XLA Ops:
  0.6 57.0 %shard_map.165 = (f32[16,128,128]{2,1,0:T(8,128)S(1)}, f32[16,128,128]{2,1,0:T(8,128)S(1)}, f32[16,128,128]{2,1,0:T(8,128)S(1)}, f32[1,128]{1,0:T(1,128)S(1)}) custom-call(f32[1,128,2048]{2,1,0:T(8,128)} %sol_h.1, f32[1,128,2048]{2,1,0:T(8,128)} %res_h.1, f32[1,128,2048]{2,1,0:T(8,128)} %dir_h.1, f32[1,128]{1,0:T(1,128)} %bitcast.1, s32[1,4]{1,0:T(1,128)} %slots_h.1, ...), custom_call_target="tpu_custom_call" | custom-call | tf_op jit(solution)/shard_map/pallas_call | solution.py:631
  57.6 2.2 %shard_map.166 = (f32[1,128,2048]{2,1,0:T(8,128)}, f32[1,128,2048]{2,1,0:T(8,128)}, f32[1,128,2048]{2,1,0:T(8,128)}, f32[128]{0:T(128)}) custom-call(f32[16,128,128]{2,1,0:T(8,128)S(1)} %get-tuple-element.8.sol, f32[16,128,128]{2,1,0:T(8,128)S(1)} %get-tuple-element.9.res, f32[16,128,128]{2,1,0:T(8,128)S(1)} %get-tuple-element.10.dirn, ...), custom_call_target="tpu_custom_call" | custom-call | tf_op jit(solution)/shard_map/pallas_call | solution.py:646

commit v4 on v3

--- a/solution.py
+++ b/solution.py
@@ -500,9 +500,6 @@
             for h in range(pieces):
                 far_copies[p, h].wait_recv()
                 column_copies.append(send(place(far, p, h), place(far, p, h), near))
-        s_sub.wait_recv()
-        join_face(0)
-        local_face(0)
         for c in column_copies:
             c.wait_recv()
     else:
@@ -513,9 +510,6 @@
                 for o in range(1, n_grp):
                     column_copies.append(send(place(mg, p, h), place(mg, p, h), grp_at(o)))
         s_sub = send(Ss.at[0], Sr.at[0], sub_at(-1))
-        s_sub.wait_recv()
-        join_face(0)
-        local_face(0)
         for c in column_copies:
             c.wait_recv()
 
@@ -532,6 +526,9 @@
     corr[...] = correction
     c_sub = send(corr, RC.at[0], sub_at(-1))
     c_grp = send(corr, RC.at[1], grp_at(-1))
+    s_sub.wait_recv()
+    join_face(0)
+    local_face(0)
     product_row = row_sums(acc[...] + correction * crs[...])
     copies = total_start(product_row, red_b)
 

time: 59.9 us -> 59.4 us (level)
  no operation moved by 1% of the time
where the time goes in v4:
time: 59.4 us; the launch traced here: 59.2 us
  Pallas kernels  58.6 us (99%)
  between operations  0.64 us (1%)
    pallas_call x1, Pallas kernels, shards(): pl.pallas_call(functools.partial(kernel, n_sub, n_grp), out_shape=(field,...  56.4 us
    pallas_call x1, Pallas kernels, shards(): pl.pallas_call(store, out_shape=(whole, whole, whole, jax.ShapeDtypeStruc...  2.16 us

profile of v4, /device:TPU:0, one launch (start us, length us, event | category | flops | bytes accessed | tf_op | source)
XLA Modules:
  0.0 59.2 jit_solution(1516312144784989132)
XLA Ops:
  0.6 56.4 %shard_map.165 = (f32[16,128,128]{2,1,0:T(8,128)S(1)}, f32[16,128,128]{2,1,0:T(8,128)S(1)}, f32[16,128,128]{2,1,0:T(8,128)S(1)}, f32[1,128]{1,0:T(1,128)S(1)}) custom-call(f32[1,128,2048]{2,1,0:T(8,128)} %sol_h.1, f32[1,128,2048]{2,1,0:T(8,128)} %res_h.1, f32[1,128,2048]{2,1,0:T(8,128)} %dir_h.1, f32[1,128]{1,0:T(1,128)} %bitcast.1, s32[1,4]{1,0:T(1,128)} %slots_h.1, ...), custom_call_target="tpu_custom_call" | custom-call | tf_op jit(solution)/shard_map/pallas_call | solution.py:628
  57.0 2.2 %shard_map.166 = (f32[1,128,2048]{2,1,0:T(8,128)}, f32[1,128,2048]{2,1,0:T(8,128)}, f32[1,128,2048]{2,1,0:T(8,128)}, f32[128]{0:T(128)}) custom-call(f32[16,128,128]{2,1,0:T(8,128)S(1)} %get-tuple-element.8.sol, f32[16,128,128]{2,1,0:T(8,128)S(1)} %get-tuple-element.9.res, f32[16,128,128]{2,1,0:T(8,128)S(1)} %get-tuple-element.10.dirn, ...), custom_call_target="tpu_custom_call" | custom-call | tf_op jit(solution)/shard_map/pallas_call | solution.py:643
